TPU v7x, 32 devices: a whole 2x2x4 slice. The times are simulated.
32 devices in a mesh: head: 4 (over z), batch: 8 (over y, x, core).
Axes of the slice: x: 2, y: 2, z: 4, core: 2. Of those that a mesh axis runs over, the one named last changes fastest.
Arguments:
- window_ids: int32 [32, 22], replicated, may hold values from 0 to 64127
- pool_ids: int32 [32, 64, 3], replicated, may hold values from 0 to 64127
- guess_index: int32 [32, 7], replicated, may hold values from 0 to 63
- lengths: int32 [32], P('batch'), may hold values from 16 to 2048, as said below
- embed_table: bfloat16 [64128, 8192], P('batch', 'head'), may hold values from -6 to 6
- w_query: bfloat16 [8192, 8192], P('batch', 'head'), may hold values from -0.0625 to 0.0625
- w_key: bfloat16 [8192, 1024], P('batch', 'head'), may hold values from -0.0625 to 0.0625
- w_value: bfloat16 [8192, 1024], P('batch', 'head'), may hold values from -0.0625 to 0.0625
- k_cache: bfloat16 [8, 32, 2048, 128], P(None, None, ('head', 'batch')), may hold values from -300 to 300
- v_cache: bfloat16 [8, 32, 2048, 128], P(None, None, ('head', 'batch')), may hold values from -12 to 12
Outputs:
- attended: bfloat16 [1376, 8192], P('batch', 'head')
- k_decode: bfloat16 [8, 32, 2048, 128], P('head', 'batch')
- v_decode: bfloat16 [8, 32, 2048, 128], P('head', 'batch')
Inputs may be any that keep to these rules, and one draw needn't show every extreme that they name: `lengths`: in every draw one sequence has exactly 2048 cached tokens.
All inputs are finite; a program needn't handle non-finite values.
Results may differ from a plain program's by a relative error of at most 0.0055.
The roundings to bfloat16 on the way count: a program that leaves them out, or rounds other values in their place, can miss the bound.
Values may be sent and summed in bfloat16 or wider, within the bound.
No kernel may reach another device: no remote copies, remote signals or barrier semaphores. Data moves between devices by JAX's collectives and lax.ppermute only.
A program may use at most 192 MiB of HBM per device.

v0:
```python
import jax
import jax.numpy as jnp
import numpy as np
from jax import lax
from jax.sharding import PartitionSpec as P

W = 7
NG = 4
G = 7


ROPE_BASE = 500000.0
NORM_EPS = 1e-05


def layout_tables():
    levels = NG - 1
    level_of = np.repeat(np.arange(levels), W)
    column_of = np.tile(np.arange(W), levels)
    window_mask = (level_of[None, :] == 0) & (column_of[None, :] <= column_of[:, None]) | (
        column_of[None, :] == column_of[:, None]
    ) & (level_of[None, :] <= level_of[:, None])
    guess_of = np.repeat(np.arange(G), levels)
    slot_of = np.tile(np.arange(levels), G)
    guess_mask = (guess_of[None, :] == guess_of[:, None]) & (slot_of[None, :] <= slot_of[:, None])
    window_rows = levels * W
    total_rows = 1 + window_rows + G * levels
    allowed = np.zeros((total_rows, total_rows), np.bool_)
    allowed[:, 0] = True
    allowed[1 : 1 + window_rows, 1 : 1 + window_rows] = window_mask
    allowed[1 + window_rows :, 1 + window_rows :] = guess_mask
    offsets = np.concatenate(
        [
            np.zeros(1, np.int32),
            (1 + level_of + column_of).astype(np.int32),
            (1 + slot_of).astype(np.int32),
        ]
    )
    return (offsets, allowed)


def gather_ids(window_ids, pool_ids, guess_index):
    wanted = jnp.broadcast_to(
        guess_index[:, :, None], (guess_index.shape[0], guess_index.shape[1], pool_ids.shape[2])
    )
    picked = jnp.take_along_axis(pool_ids, wanted, axis=1)
    return jnp.concatenate([window_ids, picked.reshape(picked.shape[0], -1)], axis=1)


def rotate(vectors, positions):
    head_dim = vectors.shape[-1]
    half_dim = head_dim // 2
    ladder = jnp.arange(half_dim).astype(jnp.float32)
    frequencies = jnp.power(ROPE_BASE, ladder * (-2.0 / head_dim))
    angles = positions.astype(jnp.float32)[..., None] * frequencies
    cosine = jnp.cos(angles)[..., None, :]
    sines = jnp.sin(angles)[..., None, :]
    front_half = vectors[..., :half_dim]
    second = vectors[..., half_dim:]
    return jnp.concatenate(
        [front_half * cosine - second * sines, second * cosine + front_half * sines], axis=-1
    )


def per_device(
    window_ids,
    pool_ids,
    guess_index,
    lengths,
    embed_table,
    w_query,
    w_key,
    w_value,
    k_cache,
    v_cache,
):
    offsets, allowed = layout_tables()
    total_rows = offsets.shape[0]
    n_head = lax.axis_size("head")
    n_batch = lax.axis_size("batch")
    kv_total, seq_total, slab, head_dim = k_cache.shape
    kv_dev = kv_total // n_head
    seq_dev = seq_total // n_batch
    token_ids = gather_ids(window_ids, pool_ids, guess_index).reshape(-1)
    vocab_rows = embed_table.shape[0]
    local_ids = token_ids - lax.axis_index("batch") * vocab_rows
    inside = (local_ids >= 0) & (local_ids < vocab_rows)
    found_rows = jnp.take(embed_table, jnp.clip(local_ids, 0, vocab_rows - 1), axis=0)
    partial_rows = jnp.where(inside[:, None], found_rows.astype(jnp.float32), 0.0)
    embedded = lax.psum_scatter(
        partial_rows.astype(jnp.bfloat16), "batch", scatter_dimension=0, tiled=True
    )
    embedded = lax.all_gather(embedded, "head", axis=1, tiled=True)
    widened = embedded.astype(jnp.float32)
    normed = (
        widened * lax.rsqrt(jnp.mean(widened * widened, axis=-1, keepdims=True) + NORM_EPS)
    ).astype(jnp.bfloat16)
    pieces = (
        lax.all_gather(w_query, "batch", axis=0, tiled=True),
        lax.all_gather(w_key, "batch", axis=0, tiled=True),
        lax.all_gather(w_value, "batch", axis=0, tiled=True),
    )
    query_raw, key_raw, value_raw = tuple(
        (jnp.dot(normed, piece_part, preferred_element_type=jnp.float32) for piece_part in pieces)
    )
    q_heads = w_query.shape[1] // head_dim
    per_group = q_heads // kv_dev
    positions = lengths[:, None] + jnp.asarray(offsets).astype(jnp.int32)[None, :]
    queries = rotate(query_raw.reshape(seq_dev, total_rows, q_heads, head_dim), positions).astype(
        jnp.bfloat16
    )
    keys_new = rotate(key_raw.reshape(seq_dev, total_rows, kv_dev, head_dim), positions).astype(
        jnp.bfloat16
    )
    values_new = value_raw.astype(jnp.bfloat16).reshape(seq_dev, total_rows, kv_dev, head_dim)

    def arrange(kv_block):
        shaped = kv_block.reshape(n_head, kv_dev, n_batch, seq_dev, slab, head_dim)
        return jnp.swapaxes(shaped, 1, 2)

    context = slab * n_head * n_batch
    flat_k = arrange(k_cache).reshape(n_head * n_batch, kv_dev, seq_dev, slab, head_dim)
    flat_v = arrange(v_cache).reshape(n_head * n_batch, kv_dev, seq_dev, slab, head_dim)
    k_here, v_here = (
        lax.all_to_all(flat_k, ("head", "batch"), split_axis=0, concat_axis=3, tiled=True),
        lax.all_to_all(flat_v, ("head", "batch"), split_axis=0, concat_axis=3, tiled=True),
    )
    k_here = k_here.reshape(kv_dev, seq_dev, context, head_dim)
    v_here = v_here.reshape(kv_dev, seq_dev, context, head_dim)
    q_five = queries.reshape(seq_dev, total_rows, kv_dev, per_group, head_dim)
    score_scale = head_dim ** (-0.5)
    old_scores = (
        jnp.einsum("stkgd,kscd->skgtc", q_five, k_here, preferred_element_type=jnp.float32)
        * score_scale
    )
    new_scores = (
        jnp.einsum("stkgd,sukd->skgtu", q_five, keys_new, preferred_element_type=jnp.float32)
        * score_scale
    )
    visible = jnp.arange(context)[None, :] < lengths[:, None]
    old_scores = jnp.where(visible[:, None, None, None, :], old_scores, -1e30)
    new_scores = jnp.where(jnp.asarray(allowed), new_scores, -1e30)
    row_peak = jnp.maximum(
        jnp.max(old_scores, axis=-1, keepdims=True), jnp.max(new_scores, axis=-1, keepdims=True)
    )
    old_powers = jnp.exp(old_scores - row_peak)
    new_powers = jnp.exp(new_scores - row_peak)
    denominator = jnp.sum(old_powers, axis=-1, keepdims=True) + jnp.sum(
        new_powers, axis=-1, keepdims=True
    )
    old_weights = (old_powers / denominator).astype(jnp.bfloat16)
    new_weights = (new_powers / denominator).astype(jnp.bfloat16)
    blended = jnp.einsum(
        "skgtc,kscd->stkgd", old_weights, v_here, preferred_element_type=jnp.float32
    )
    blended = blended + jnp.einsum(
        "skgtu,sukd->stkgd", new_weights, values_new, preferred_element_type=jnp.float32
    )
    attended = blended.astype(jnp.bfloat16).reshape(seq_dev * total_rows, q_heads * head_dim)
    return (attended, k_here, v_here)


def solution(mesh):
    placed = (
        P(),
        P(),
        P(),
        P("batch"),
        P("batch", "head"),
        P("batch", "head"),
        P("batch", "head"),
        P("batch", "head"),
        P(None, None, ("head", "batch"), None),
        P(None, None, ("head", "batch"), None),
    )
    return jax.shard_map(
        per_device,
        mesh=mesh,
        in_specs=placed,
        out_specs=(
            P("batch", "head"),
            P("head", "batch", None, None),
            P("head", "batch", None, None),
        ),
        check_vma=False,
    )
```

profile of v0, /device:TPU:0, one launch (start us, length us, event | category | flops | bytes accessed | tf_op | source)
XLA Modules:
  0.0 621.0 jit_solution(6536742778525920510)
XLA Ops:
  7.9 0.8 copy.112
  10.0 9.1 %gather_fusion.1 = s32[672]{0:T(1024)S(1)} fusion(s32[32,64,3]{1,0,2:T(8,128)S(1)} %copy-done, s32[672]{0:T(1024)S(1)} %reshape.206), kind=kCustom, calls=%fused_computation.1 | custom fusion | bytes 13440 | tf_op jit(solution)/shard_map/jit(take_along_axis)/gather | solution.py:46
  20.2 53.6 %gather_fusion = bf16[1376,2048]{1,0:T(8,128)(2,1)} fusion(bf16[8016,2048]{1,0:T(8,128)(2,1)} %param.16, s32[2048]{0:T(1024)S(1)} %pad_clamp_fusion), kind=kCustom, calls=%fused_computation | custom fusion | bytes 11277696 | tf_op jit(solution)/shard_map/jit(_take)/gather | solution.py:88
  73.7 7.0 %select_convert_fusion = bf16[1376,2048]{1,0:T(8,128)(2,1)} fusion(bf16[1376,2048]{1,0:T(8,128)(2,1)} %gather_fusion, pred[1376]{0:T(1024)(128)(4,1)S(1)} %compare_and_fusion.1, pred[1376]{0:T(1024)(128)(4,1)S(1)} %and.29), kind=kLoop, calls=%fused_computation.8 | loop fusion | flops 11272192 | bytes 11274944 | tf_op jit(solution)/shard_map/convert_element_type | solution.py:91
  80.7 63.5 %fusion = bf16[176,2048]{1,0:T(8,128)(2,1)S(1)} fusion(bf16[1376,2048]{1,0:T(8,128)(2,1)} %select_convert_fusion), kind=kCustom, calls=%all-reduce-scatter | all-reduce-scatter fusion | flops 2883585 | bytes 6357504
  144.3 1.3 collective-permute-start
  146.9 1.5 concatenate.25
  148.3 1.0 constant_dynamic-slice_fusion
  149.5 0.7 all-gather.9.cloned.1.call-update
  151.5 5.6 copy.121
  157.1 9.4 %all-to-all-start = ((bf16[32,2,4,64,128]{4,3,1,2,0:T(8,128)(2,1)}), bf16[32,2,4,64,128]{4,3,1,2,0:T(8,128)(2,1)}, u32[]{:S(2)}, u32[]{:S(2)}) async-start(bf16[32,2,4,64,128]{4,3,1,2,0:T(8,128)(2,1)} %bitcast.80), calls=%async_computation | async-start | bytes 8388608 | tf_op jit(solution)/shard_map/all_to_all | solution.py:125
  166.4 5.6 copy.130
  172.0 130.5 %all-to-all-done = bf16[32,2,4,64,128]{4,3,1,2,0:T(8,128)(2,1)} async-done(((bf16[32,2,4,64,128]{4,3,1,2,0:T(8,128)(2,1)}), bf16[32,2,4,64,128]{4,3,1,2,0:T(8,128)(2,1)}, u32[]{:S(2)}, u32[]{:S(2)}) %all-to-all-start) | async-done | bytes 4194336 | tf_op jit(solution)/shard_map/all_to_all | solution.py:125
  302.5 3.9 all-to-all-start.1
  307.1 2.6 fusion.4
  309.6 28.7 %all-gather.9.cloned.1.call-done = bf16[8192,256]{1,0:T(8,128)(2,1)} async-done(((bf16[1024,256]{1,0:T(8,128)(2,1)}), bf16[8192,256]{1,0:T(8,128)(2,1)}) %all-gather.9.cloned.1.call-update) | async-done | bytes 4194320 | tf_op jit(solution)/shard_map/all_gather | solution.py:100
  338.4 4.0 fusion.25
  342.5 57.4 %all-gather.11.cloned.1.call-done = bf16[8192,256]{1,0:T(8,128)(2,1)} async-done(((bf16[1024,256]{1,0:T(8,128)(2,1)}), bf16[8192,256]{1,0:T(8,128)(2,1)}) %all-gather.11.cloned.1.call-update) | async-done | bytes 4194320 | tf_op jit(solution)/shard_map/all_gather | solution.py:101
  399.9 3.2 convolution_convert_fusion
  403.4 6.0 copy.122
  409.4 4.2 copy.131
  413.7 0.7 copy-done.2
  414.4 2.7 copy.135
  417.7 2.3 copy.136
  420.0 141.8 %all-gather.7.cloned.1.call-done = bf16[8192,2048]{1,0:T(8,128)(2,1)} async-done(((bf16[1024,2048]{1,0:T(8,128)(2,1)}), bf16[8192,2048]{1,0:T(8,128)(2,1)}) %all-gather.7.cloned.1.call-update) | async-done | bytes 33554448 | tf_op jit(solution)/shard_map/all_gather | solution.py:99
  561.8 13.7 %fusion.27 = f32[172,2048]{1,0:T(8,128)S(1)} fusion(bf16[8192,2048]{1,0:T(8,128)(2,1)} %all-gather.7.cloned.1.call-done, bf16[172,8192]{1,0:T(8,128)(2,1)S(1)} %copy-done.5, f32[172]{0:T(256)S(1)} %add_rsqrt_fusion), kind=kOutput, calls=%fused_computation.63 | convolution fusion | flops 5775589376 | bytes 37782192 | tf_op jit(solution)/shard_map/dot_general | solution.py:104
  577.0 1.0 copy-done.3
  578.0 9.3 %bitcast_reduce_fusion = (f32[4,2,8,43]{2,3,1,0:T(8,128)S(1)}, f32[4,2,43,8,2048]{4,3,2,1,0:T(8,128)}) fusion(pred[4,2048]{1,0:T(4,128)(4,1)S(1)} %iota_compare_fusion, bf16[2,4,2048,128,1]{3,2,4,0,1:T(8,128)(2,1)S(1)} %bitcast.76, bf16[4,43,2,8,128]{4,3,2,1,0:T(8,128)(2,1)S(1)} %pad_maximum_fusion), kind=kOutput, calls=%fused_computation.3 | convolution fusion | flops 1459746048 | bytes 27462400 | tf_op jit(solution)/shard_map/stkgd,kscd->skgtc/dot_general | solution.py:133
  587.4 1.0 fusion.30
  589.0 10.9 %fusion.2 = f32[4,2,8,43]{2,3,1,0:T(8,128)S(1)} fusion(f32[4,2,43,8,2048]{4,3,2,1,0:T(8,128)} %get-tuple-element.27, f32[4,2,8,43]{2,3,1,0:T(8,128)S(1)} %copy.127, pred[4,2048]{1,0:T(4,128)(4,1)S(1)} %iota_compare_fusion), kind=kLoop, calls=%fused_computation.7 | loop fusion | flops 22541632 | bytes 22574592 | tf_op jit(solution)/shard_map/reduce_sum | solution.py:148
  601.1 11.5 %fusion.7 = f32[4,43,2,8,128]{4,3,1,2,0:T(8,128)S(1)} fusion(bf16[2,4,2048,128,1]{3,2,4,0,1:T(8,128)(2,1)} %bitcast.78, f32[4,2,43,8,2048]{4,3,2,1,0:T(8,128)} %get-tuple-element.27, f32[4,2,8,43]{2,3,1,0:T(8,128)S(1)} %copy.129, f32[4,2,8,43]{2,3,1,0:T(8,128)S(1)} %copy.127, pred[4,2048]{1,0:T(4,128)(4,1)S(1)} %iota_compare_fusion), kind=kOutput, calls=%fused_computation.19 | convolution fusion | flops 1471021056 | bytes 28177920 | tf_op jit(solution)/shard_map/skgtc,kscd->stkgd/dot_general | solution.py:153
  613.3 1.2 reshape.197
  (74 shorter events, 10.6 us)
Async XLA Ops:
  7.2 2.8 copy-start
  7.2 299.9 %all-gather.5.cloned.1.call-start = ((), (), s32[]{:S(2)}) async-start(), calls=%async_computation.2 | async-start | bytes 3604480 | tf_op jit(solution)/shard_map/all_gather | solution.py:93
  10.0 9.6 %copy-start.6 = (s32[32,22]{0,1:T(8,128)S(1)}, s32[32,22]{0,1:T(8,128)}, u32[]{:S(2)}) copy-start(s32[32,22]{0,1:T(8,128)} %param.12) | copy-start | bytes 8452
  80.7 64.9 %copy-start.9 = (u32[32]{0:T(128)S(1)}, u32[32]{0:T(128)}, u32[]{:S(2)}) copy-start(u32[32]{0:T(128)} %constant.86) | copy-start | bytes 388
  144.3 2.6 collective-permute-start
  149.4 189.0 %all-gather.9.cloned.1.call-start = ((), (), s32[]{:S(2)}) async-start(), calls=%async_computation.4 | async-start | bytes 4718592 | tf_op jit(solution)/shard_map/all_gather | solution.py:100
  150.2 249.8 %all-gather.11.cloned.1.call-start = ((), (), s32[]{:S(2)}) async-start(), calls=%async_computation.5 | async-start | bytes 4718592 | tf_op jit(solution)/shard_map/all_gather | solution.py:101
  150.9 410.9 %all-gather.7.cloned.1.call-start = ((), (), s32[]{:S(2)}) async-start(), calls=%async_computation.3 | async-start | bytes 37748736 | tf_op jit(solution)/shard_map/all_gather | solution.py:99
  157.1 145.4 %all-to-all-start = ((bf16[32,2,4,64,128]{4,3,1,2,0:T(8,128)(2,1)}), bf16[32,2,4,64,128]{4,3,1,2,0:T(8,128)(2,1)}, u32[]{:S(2)}, u32[]{:S(2)}) async-start(bf16[32,2,4,64,128]{4,3,1,2,0:T(8,128)(2,1)} %bitcast.80), calls=%async_computation | async-start | bytes 8388608 | tf_op jit(solution)/shard_map/all_to_all | solution.py:125
  302.5 3.9 copy-start.8
  302.5 3.9 copy-start.10
  302.5 106.9 %all-to-all-start.1 = ((bf16[32,2,4,64,128]{4,3,1,2,0:T(8,128)(2,1)}), bf16[32,2,4,64,128]{4,3,1,2,0:T(8,128)(2,1)}, u32[]{:S(2)}, u32[]{:S(2)}) async-start(bf16[32,2,4,64,128]{4,3,1,2,0:T(8,128)(2,1)} %bitcast.79), calls=%async_computation.1 | async-start | bytes 8388608 | tf_op jit(solution)/shard_map/all_to_all | solution.py:126
  309.6 90.3 %copy-start.5 = (bf16[172,8192]{1,0:T(8,128)(2,1)S(1)}, bf16[172,8192]{1,0:T(8,128)(2,1)}, u32[]{:S(2)}) copy-start(bf16[172,8192]{1,0:T(8,128)(2,1)} %all-gather.5.cloned.1.call-done) | copy-start | bytes 8454148
  409.4 5.0 copy-start.2
  413.7 4.0 copy-start.4
  575.8 2.2 copy-start.3
  578.0 9.4 %copy-start.7 = (pred[43,43]{0,1:T(8,128)(4,1)S(1)}, pred[43,43]{0,1:T(8,128)(4,1)}, u32[]{:S(2)}) copy-start(pred[43,43]{0,1:T(8,128)(4,1)} %constant.63.clone) | copy-start | bytes 5551
  601.1 13.4 %copy-start.1 = (s32[32,64,3]{1,0,2:T(8,128)S(1)}, s32[32,64,3]{1,0,2:T(8,128)}, u32[]{:S(2)}) copy-start(s32[32,64,3]{1,0,2:T(8,128)} %param.13) | copy-start | bytes 73732
Sparse Core Ops, SparseCore 0:
  149.5 121.1 all-gather.4
  272.6 65.6 all-gather.8
  340.3 59.6 all-gather.10
  401.7 160.0 all-gather.6
where the time goes:
time: 622 us; the launch traced here: 621 us
  waiting for transfers between devices  360 us (58%)
  local copies, waits for them, and re-layouts  99.5 us (16%)
  blocking collectives  63.5 us (10%)
  matrix products  43.3 us (7%)
  other arithmetic  24.8 us (4%)
  between operations  14.8 us (2%)
  starting transfers between devices  14.7 us (2%)
    all_gather x1, waiting for transfers between devices, per_device(): lax.all_gather(w_query, 'batch', axis=0, tiled=True)  142 us
    all_to_all x1, waiting for transfers between devices, per_device(): lax.all_to_all(flat_k, ('head', 'batch'), split_axis=0, concat_axis=3, ti...  130 us
    unnamed x1, blocking collectives  63.5 us
    all_gather x1, waiting for transfers between devices, per_device(): lax.all_gather(w_value, 'batch', axis=0, tiled=True)  57.4 us
    gather x1, local copies, waits for them, and re-layouts, per_device(): jnp.take(embed_table, jnp.clip(local_ids, 0, vocab_rows - 1), axis=0)  53.6 us
    all_gather x1, waiting for transfers between devices, per_device(): lax.all_gather(w_key, 'batch', axis=0, tiled=True)  28.7 us
    dot_general x3, matrix products, per_device(): jnp.dot(normed, piece_part, preferred_element_type=jnp.float32)  20.9 us
  transfers between devices with their start and end apart: 7, of which 4 were waited for; matrix products, arithmetic and copies ran while one was open for 6% of the time, Pallas kernels for 0%

commit v1 on v0

v1 whole, which is shorter than its diff:
```python
import jax
import jax.numpy as jnp
import numpy as np
from jax import lax
from jax.experimental import pallas as pl
from jax.experimental.pallas import tpu as pltpu
from jax.sharding import PartitionSpec as P


W = 7
NG = 4
G = 7

ROPE_BASE = 500000.0
NORM_EPS = 1e-05
SLOTS = 32
UNROLL = 4
CHUNK = 512
SUM_TYPE = jnp.float16


def layout_tables():
    levels = NG - 1
    level_of = np.repeat(np.arange(levels), W)
    column_of = np.tile(np.arange(W), levels)
    window_mask = (level_of[None, :] == 0) & (column_of[None, :] <= column_of[:, None]) | (
        column_of[None, :] == column_of[:, None]
    ) & (level_of[None, :] <= level_of[:, None])
    guess_of = np.repeat(np.arange(G), levels)
    slot_of = np.tile(np.arange(levels), G)
    guess_mask = (guess_of[None, :] == guess_of[:, None]) & (slot_of[None, :] <= slot_of[:, None])
    window_rows = levels * W
    total_rows = 1 + window_rows + G * levels
    allowed = np.zeros((total_rows, total_rows), np.bool_)
    allowed[:, 0] = True
    allowed[1 : 1 + window_rows, 1 : 1 + window_rows] = window_mask
    allowed[1 + window_rows :, 1 + window_rows :] = guess_mask
    offsets = np.concatenate(
        [
            np.zeros(1, np.int32),
            (1 + level_of + column_of).astype(np.int32),
            (1 + slot_of).astype(np.int32),
        ]
    )
    return (offsets, allowed)


def round_up(value, unit):
    return -(-value // unit) * unit


def lookup_rows(window_ids, pool_ids, guess_index, embed_table, n_batch, rows_seq):
    seqs, window = window_ids.shape
    guesses = guess_index.shape[1]
    pool, levels = pool_ids.shape[1:]
    seq_dev = seqs // n_batch
    vocab_rows, width = embed_table.shape
    group_rows = seq_dev * rows_seq
    half = (n_batch // 2) * group_rows
    table = embed_table.reshape(vocab_rows // 8, 8, width)
    most = n_batch * group_rows

    def kernel(me_ref, window_ref, pool_ref, guess_ref, table_ref, even_ref, odd_ref, rows, held, where_to, which, sems):
        me = me_ref[0]
        first = me * vocab_rows

        def clear(i, _):
            rows[pl.ds(pl.multiple_of(i * 8, 8), 8), :] = jnp.zeros((8, width), jnp.float32)
            return 0

        lax.fori_loop(0, most // 8, clear, 0)

        def note(token, row, found):
            local = token - first
            where_to[found] = row
            which[found] = local
            return found + jnp.where(jnp.logical_and(local >= 0, local < vocab_rows), 1, 0)

        def scan(seq, found):
            step = jnp.bitwise_xor(seq // seq_dev, me)
            place = (step % 2) * (n_batch // 2) + step // 2
            base = place * group_rows + (seq % seq_dev) * rows_seq
            for i in range(window):
                found = note(window_ref[seq, i], base + i, found)
            for g in range(guesses):
                at = guess_ref[seq, g] * levels
                for j in range(levels):
                    found = note(pool_ref[seq, at + j], base + window + g * levels + j, found)
            return found

        found = lax.fori_loop(0, seqs, scan, 0)

        for n in range(UNROLL):
            where_to[found + n] = most
            which[found + n] = 0
        groups = (found + UNROLL - 1) // UNROLL

        def fetch(i, slot):
            return pltpu.make_async_copy(
                table_ref.at[lax.shift_right_logical(which[i], 3)], held.at[slot], sems.at[slot]
            )

        def prime(i, _):
            for n in range(UNROLL):
                fetch(i * UNROLL + n, i * UNROLL + n).start()
            return 0

        lax.fori_loop(0, jnp.minimum(groups, SLOTS // UNROLL), prime, 0)
        sub = lax.broadcasted_iota(jnp.int32, (8, width), 0)

        def take(i, _):
            slot = lax.rem(i, SLOTS // UNROLL) * UNROLL
            for n in range(UNROLL):
                fetch(i * UNROLL + n, slot + n).wait()
            for n in range(UNROLL):
                source, target = which[i * UNROLL + n], where_to[i * UNROLL + n]
                low = jnp.bitwise_and(target, 7)
                tile = held[slot + n].astype(jnp.float32)
                turned = pltpu.roll(tile, jnp.bitwise_and(low - source, 7), 0)
                at = pl.ds(pl.multiple_of(target - low, 8), 8)
                rows[at, :] = jnp.where(sub == low, turned, rows[at, :])

            @pl.when(i + SLOTS // UNROLL < groups)
            def _():
                for n in range(UNROLL):
                    fetch((i + SLOTS // UNROLL) * UNROLL + n, slot + n).start()

            return 0

        lax.fori_loop(0, groups, take, 0)

        def narrow(i, _):
            at = pl.multiple_of(i * 16, 16)
            even_ref[pl.ds(at, 16), :] = rows[pl.ds(at, 16), :].astype(jnp.bfloat16)
            odd_ref[pl.ds(at, 16), :] = rows[pl.ds(at + half, 16), :].astype(jnp.bfloat16)
            return 0

        lax.fori_loop(0, half // 16, narrow, 0)

    smem = pl.BlockSpec(memory_space=pltpu.SMEM)
    vmem = pl.BlockSpec(memory_space=pltpu.VMEM)
    out = jax.ShapeDtypeStruct((half, width), jnp.bfloat16)
    me = lax.axis_index("batch").astype(jnp.int32).reshape(1)
    even, odd = pl.pallas_call(
        kernel,
        out_shape=(out, out),
        in_specs=[smem, smem, smem, smem, pl.BlockSpec(memory_space=pltpu.HBM)],
        out_specs=(vmem, vmem),
        scratch_shapes=[
            pltpu.VMEM((most + 8, width), jnp.float32),
            pltpu.VMEM((SLOTS, 8, width), jnp.bfloat16),
            pltpu.SMEM((most + 8,), jnp.int32),
            pltpu.SMEM((most + 8,), jnp.int32),
            pltpu.SemaphoreType.DMA((SLOTS,)),
        ],
        cost_estimate=pl.CostEstimate(flops=10_000_000_000, bytes_accessed=20_000_000, transcendentals=0),
        name="lookup",
    )(me, window_ids, pool_ids.reshape(seqs, pool * levels), guess_index, table)
    shape = (n_batch // 2, group_rows, width)
    return even.reshape(shape), odd.reshape(shape)


def score_head(k, qkv, visible_new, lengths, k_got, kv_dev, per_group, earlier):
    senders, seq_dev, slab, head_dim = k_got.shape
    context = senders * slab
    chunk = min(CHUNK, context)
    chunks = context // chunk
    part = chunk // slab
    rows_pad = qkv.shape[1]
    rows = per_group * rows_pad
    q_cols = per_group * head_dim
    scale = head_dim ** (-0.5)
    f32, bf16 = jnp.float32, jnp.bfloat16
    dims = (((1,), (1,)), ((), ()))
    plain = (((1,), (0,)), ((), ()))

    def kernel(len_ref, q_ref, kn_ref, vn_ref, mask_ref, k_ref, *refs):
        w_ref, new_ref, ko_ref, q_all, score, peak, total = refs[-7:]
        length = len_ref[pl.program_id(0)]
        for g in range(per_group):
            q_all[pl.ds(g * rows_pad, rows_pad), :] = q_ref[0, :, pl.ds(g * head_dim, head_dim)]
        k_new, v_new = kn_ref[0], vn_ref[0]
        s_new = lax.dot_general(q_all[...], k_new, dims, preferred_element_type=f32) * scale
        s_new = jnp.where(mask_ref[...] > 0, s_new, -1e30)
        peak[...] = jnp.max(s_new, axis=-1, keepdims=True)
        for i in range(chunks):
            ko_ref[0, 0, pl.ds(i * chunk, chunk), :] = k_ref[pl.ds(i * part, part), 0].reshape(chunk, head_dim)

        for i in range(chunks):

            @pl.when(i * chunk < length)
            def _(i=i):
                got = lax.dot_general(
                    q_all[...], ko_ref[0, 0, pl.ds(i * chunk, chunk), :], dims, preferred_element_type=f32
                ) * scale
                at = lax.broadcasted_iota(jnp.int32, (rows, chunk), 1) + i * chunk
                got = jnp.where(at < length, got, -1e30)
                score[i] = got
                peak[...] = jnp.maximum(peak[...], jnp.max(got, axis=-1, keepdims=True))

        p_new = jnp.exp(s_new - peak[...])
        total[...] = jnp.sum(p_new, axis=-1, keepdims=True)
        for i in range(chunks):

            @pl.when(i * chunk < length)
            def _(i=i):
                p = jnp.exp(score[i] - peak[...])
                score[i] = p
                total[...] += jnp.sum(p, axis=-1, keepdims=True)

        inverse = 1.0 / total[...]
        new_ref[0] = lax.dot_general((p_new * inverse).astype(bf16), v_new, plain, preferred_element_type=f32)
        for i in range(chunks):

            @pl.when(i * chunk < length)
            def _(i=i):
                w_ref[0, i] = (score[i] * inverse).astype(bf16)

    heads = per_group * kv_dev
    extra = [] if earlier is None else [earlier]
    return pl.pallas_call(
        kernel,
        grid=(seq_dev,),
        out_shape=(
            jax.ShapeDtypeStruct((seq_dev, chunks, rows, chunk), bf16),
            jax.ShapeDtypeStruct((seq_dev, rows, head_dim), f32),
            jax.ShapeDtypeStruct((kv_dev, seq_dev, context, head_dim), bf16),
        ),
        in_specs=[
            pl.BlockSpec(memory_space=pltpu.SMEM),
            pl.BlockSpec((1, rows_pad, q_cols), lambda s: (s, 0, k)),
            pl.BlockSpec((1, rows_pad, head_dim), lambda s: (s, 0, heads + k)),
            pl.BlockSpec((1, rows_pad, head_dim), lambda s: (s, 0, heads + kv_dev + k)),
            pl.BlockSpec((rows, rows_pad), lambda s: (0, 0)),
            pl.BlockSpec((senders, 1, slab, head_dim), lambda s: (0, s, 0, 0)),
        ]
        + [pl.BlockSpec(memory_space=pl.ANY)] * len(extra),
        out_specs=(
            pl.BlockSpec((1, chunks, rows, chunk), lambda s: (s, 0, 0, 0)),
            pl.BlockSpec((1, rows, head_dim), lambda s: (s, 0, 0)),
            pl.BlockSpec((1, 1, context, head_dim), lambda s: (k, s, 0, 0)),
        ),
        scratch_shapes=[
            pltpu.VMEM((rows, head_dim), bf16),
            pltpu.VMEM((chunks, rows, chunk), f32),
            pltpu.VMEM((rows, 1), f32),
            pltpu.VMEM((rows, 1), f32),
        ],
        input_output_aliases={6: 2} if extra else {},
        cost_estimate=pl.CostEstimate(flops=2_000_000_000, bytes_accessed=10_000_000, transcendentals=4_000_000),
        name="score",
    )(lengths, qkv, qkv, qkv, visible_new, k_got, *extra)


def blend_head(k, weights, new_part, lengths, hi, v_got, kv_dev, per_group, rows_pad, earlier):
    n_head = len(v_got)
    senders, seq_dev, slab, head_dim = v_got[0].shape
    chunks, rows, chunk = weights.shape[1:]
    part = senders * slab
    context = n_head * part
    q_cols = per_group * head_dim
    f32, bf16 = jnp.float32, jnp.bfloat16
    plain = (((1,), (0,)), ((), ()))

    def kernel(len_ref, at_ref, w_ref, new_ref, *refs):
        o_ref, vo_ref, acc = refs[-3:]
        length = len_ref[pl.program_id(0)]
        acc[...] = new_ref[0]
        for d in range(n_head):
            at = lax.rem(at_ref[0] + n_head - d, n_head) * part
            vo_ref[0, 0, pl.ds(pl.multiple_of(at, part), part), :] = refs[d][:, 0].reshape(part, head_dim)
        for i in range(chunks):

            @pl.when(i * chunk < length)
            def _(i=i):
                acc[...] += lax.dot_general(
                    w_ref[0, i], vo_ref[0, 0, pl.ds(i * chunk, chunk), :], plain, preferred_element_type=f32
                )

        for g in range(per_group):
            o_ref[0, :, pl.ds(g * head_dim, head_dim)] = acc[pl.ds(g * rows_pad, rows_pad), :].astype(bf16)

    extra = [] if earlier is None else list(earlier)
    return pl.pallas_call(
        kernel,
        grid=(seq_dev,),
        out_shape=(
            jax.ShapeDtypeStruct((seq_dev, rows_pad, kv_dev * q_cols), bf16),
            jax.ShapeDtypeStruct((kv_dev, seq_dev, context, head_dim), bf16),
        ),
        in_specs=[
            pl.BlockSpec(memory_space=pltpu.SMEM),
            pl.BlockSpec(memory_space=pltpu.SMEM),
            pl.BlockSpec((1, chunks, rows, chunk), lambda s: (s, 0, 0, 0)),
            pl.BlockSpec((1, rows, head_dim), lambda s: (s, 0, 0)),
        ]
        + [pl.BlockSpec((senders, 1, slab, head_dim), lambda s: (0, s, 0, 0))] * n_head
        + [pl.BlockSpec(memory_space=pl.ANY)] * len(extra),
        out_specs=(
            pl.BlockSpec((1, rows_pad, q_cols), lambda s: (s, 0, k)),
            pl.BlockSpec((1, 1, context, head_dim), lambda s: (k, s, 0, 0)),
        ),
        scratch_shapes=[pltpu.VMEM((rows, head_dim), f32)],
        input_output_aliases={4 + n_head: 0, 5 + n_head: 1} if extra else {},
        cost_estimate=pl.CostEstimate(flops=1_000_000_000, bytes_accessed=10_000_000, transcendentals=0),
        name="blend",
    )(lengths, hi.astype(jnp.int32).reshape(1), weights, new_part, *v_got, *extra)


def pack_head(cache, k, n_head):
    kv_total, seqs, slab, head_dim = cache.shape
    kv_dev = kv_total // n_head

    def kernel(in_ref, out_ref):
        out_ref[...] = in_ref[...]

    return pl.pallas_call(
        kernel,
        grid=(n_head,),
        out_shape=jax.ShapeDtypeStruct((n_head, seqs, slab, head_dim), cache.dtype),
        in_specs=[pl.BlockSpec((1, seqs, slab, head_dim), lambda h: (h * kv_dev + k, 0, 0, 0))],
        out_specs=pl.BlockSpec((1, seqs, slab, head_dim), lambda h: (h, 0, 0, 0)),
        cost_estimate=pl.CostEstimate(flops=2_000_000_000, bytes_accessed=4_000_000, transcendentals=0),
        name="pack",
    )(cache)


def pack_sequences(cache, n_batch):
    kv_total, seqs, slab, head_dim = cache.shape
    seq_dev = seqs // n_batch

    def kernel(in_ref, out_ref):
        out_ref[0] = in_ref[...]

    return pl.pallas_call(
        kernel,
        grid=(n_batch,),
        out_shape=jax.ShapeDtypeStruct((n_batch, kv_total, seq_dev, slab, head_dim), cache.dtype),
        in_specs=[pl.BlockSpec((kv_total, seq_dev, slab, head_dim), lambda b: (0, b, 0, 0))],
        out_specs=pl.BlockSpec((1, kv_total, seq_dev, slab, head_dim), lambda b: (b, 0, 0, 0, 0)),
        cost_estimate=pl.CostEstimate(flops=4_000_000_000, bytes_accessed=8_000_000, transcendentals=0),
        name="packs",
    )(cache)


def finish_rows(halves, cosine, sines, seq_dev, rows_seq, rows_pad, q_heads, kv_dev):
    head_dim = cosine.shape[-1]
    cut = halves[0].shape[1]
    width = cut + halves[1].shape[1]
    bf16 = jnp.bfloat16

    def kernel(sum_a, sum_b, cos_ref, sin_ref, out_ref):
        for s in range(seq_dev):
            c, t = cos_ref[s], sin_ref[s]
            out_ref[s, pl.ds(rows_pad - 16, 16), :] = jnp.zeros((16, width), bf16)
            rows = pl.ds(s * rows_seq, rows_seq)
            for head in range(width // head_dim):
                at = head * head_dim
                total, at = (sum_a, at) if at < cut else (sum_b, at - cut)
                x = total[rows, pl.ds(at, head_dim)]
                if head < q_heads + kv_dev:
                    x = x * c[:rows_seq] + pltpu.roll(x, head_dim // 2, 1) * t[:rows_seq]
                out_ref[s, pl.ds(0, rows_seq), pl.ds(head * head_dim, head_dim)] = x.astype(bf16)

    vmem = pl.BlockSpec(memory_space=pltpu.VMEM)
    return pl.pallas_call(
        kernel,
        out_shape=jax.ShapeDtypeStruct((seq_dev, rows_pad, width), bf16),
        in_specs=[vmem] * 4,
        out_specs=vmem,
        cost_estimate=pl.CostEstimate(flops=2_000_000_000, bytes_accessed=4_000_000, transcendentals=0),
        name="finish",
    )(*halves, cosine, sines)


def norm_pieces(sources, hi, bi, n_head, n_batch):
    rows, width = sources[0].shape
    depth = n_head * width // n_batch
    per_plane = width // depth
    f32, bf16 = jnp.float32, jnp.bfloat16

    def kernel(at_ref, *refs):
        ins = refs[: len(sources)]
        outs = refs[len(sources) : len(sources) + n_batch]
        wide, inverse = refs[-2:]
        h, b = at_ref[0], at_ref[1]
        for d in range(1 - n_head, n_head):
            p = h - d

            @pl.when(jnp.logical_and(p >= 0, p < n_head))
            def _(d=d, p=p):
                wide[p] = ins[d + n_head - 1][...]

        squares = jnp.zeros((rows, 1), f32)
        for p in range(n_head):
            x = wide[p].astype(f32)
            squares += jnp.sum(x * x, axis=-1, keepdims=True)
        inverse[...] = lax.rsqrt(squares / (n_head * width) + NORM_EPS)
        for s in range(n_batch):
            j = jnp.bitwise_xor(b, s)
            at = pl.multiple_of((j % per_plane) * depth, depth)
            outs[s][...] = (wide[j // per_plane, :, pl.ds(at, depth)].astype(f32) * inverse[...]).astype(bf16)

    vmem = pl.BlockSpec(memory_space=pltpu.VMEM)
    return pl.pallas_call(
        kernel,
        out_shape=tuple(jax.ShapeDtypeStruct((rows, depth), bf16) for _ in range(n_batch)),
        in_specs=[pl.BlockSpec(memory_space=pltpu.SMEM)] + [vmem] * len(sources),
        out_specs=(vmem,) * n_batch,
        scratch_shapes=[pltpu.VMEM((n_head, rows, width), bf16), pltpu.VMEM((rows, 1), f32)],
        cost_estimate=pl.CostEstimate(flops=2_000_000_000, bytes_accessed=8_000_000, transcendentals=0),
        name="norm",
    )(jnp.stack([hi, bi]).astype(jnp.int32), *sources)


def layer(
    window_ids,
    pool_ids,
    guess_index,
    lengths,
    embed_table,
    w_query,
    w_key,
    w_value,
    k_cache,
    v_cache,
):
    offsets, allowed = layout_tables()
    total_rows = offsets.shape[0]
    n_head = lax.axis_size("head")
    n_batch = lax.axis_size("batch")
    kv_total, seq_total, slab, head_dim = k_cache.shape
    kv_dev = kv_total // n_head
    seq_dev = seq_total // n_batch
    hi = lax.axis_index("head")
    bi = lax.axis_index("batch")
    f32 = jnp.float32

    def exchange(cache, k):
        shaped = pack_head(cache, k, n_head).reshape(n_head * n_batch, seq_dev, slab, head_dim)
        return lax.all_to_all(shaped, ("head", "batch"), split_axis=0, concat_axis=0, tiled=True)

    k_got = [exchange(k_cache, k) for k in range(kv_dev)]

    v_packed = pack_sequences(v_cache, n_batch)
    v_near = lax.all_to_all(v_packed, "batch", split_axis=0, concat_axis=0, tiled=True)
    v_near = v_near.reshape(n_batch, n_head, kv_dev, seq_dev, slab, head_dim)
    v_got = []
    for k in range(kv_dev):
        v_got.append([])
        for d in range(n_head):
            ours = lax.dynamic_index_in_dim(v_near[:, :, k], (hi + d) % n_head, 1, keepdims=False)
            shift = [(i, (i + d) % n_head) for i in range(n_head)]
            v_got[k].append(lax.ppermute(ours, "head", shift) if d else ours)

    def swap(block, step):
        return lax.ppermute(block, "batch", [(i, i ^ step) for i in range(n_batch)])

    def halve(blocks, bits, send=lambda t: t, keep=lambda t: t):
        arr = blocks
        for n, bit in enumerate(bits):
            low = 1 << sorted(bits[n:]).index(bit)
            shape = arr.shape
            arr = arr.reshape((shape[0] // (2 * low), 2, low) + shape[1:])
            out = send(arr[:, 1])
            got = swap(out, bit)
            arr = keep(arr[:, 0]) + keep(got)
            arr = arr.reshape((shape[0] // 2,) + shape[1:])
        return arr[0]

    bits = [1 << i for i in range(n_batch.bit_length() - 1)]
    rows_seq = total_rows + 1
    group_rows = seq_dev * rows_seq

    even, odd = lookup_rows(window_ids, pool_ids, guess_index, embed_table, n_batch, rows_seq)
    merged = even + swap(odd, 1)
    cut = merged.shape[-1] // 2
    mine = jnp.concatenate(
        [halve(merged[..., :cut], bits[1:]), halve(merged[..., cut:], bits[:0:-1])],
        axis=-1,
    )

    right = [(i, i + 1) for i in range(n_head - 1)]
    left = [(i + 1, i) for i in range(n_head - 1)]
    up, down = [mine], [mine]
    for _ in range(1, n_head):
        up.append(lax.ppermute(up[-1], "head", right))
        down.append(lax.ppermute(down[-1], "head", left))
    pieces = norm_pieces(down[:0:-1] + [mine] + up[1:], hi, bi, n_head, n_batch)

    parts = [pieces[0]] + [None] * (n_batch - 1)
    for step in range(n_batch - 1, 0, -1):
        parts[step] = swap(pieces[step], step)

    weights = jnp.concatenate([w_query, w_key, w_value], axis=1)

    def project(blocks):
        stacked = jnp.concatenate(blocks, axis=0)
        done = jnp.dot(stacked, weights, preferred_element_type=f32)
        return done.reshape(len(blocks), group_rows, weights.shape[1])

    narrow, widen = (lambda t: t.astype(SUM_TYPE)), (lambda t: t.astype(f32))
    odd_part = narrow(project(parts[1::2]))
    odd_got = widen(swap(odd_part, 1))
    summed = project(parts[0::2]) + odd_got
    cut = weights.shape[1] // (2 * head_dim) * head_dim
    halves = (halve(summed[..., :cut], bits[1:], narrow, widen), halve(summed[..., cut:], bits[:0:-1], narrow, widen))

    rows_pad = round_up(rows_seq, 16)
    offsets_pad = np.zeros(rows_pad, np.int32)
    offsets_pad[:total_rows] = offsets
    positions = lengths[:, None] + jnp.asarray(offsets_pad)[None, :]
    half_dim = head_dim // 2
    ladder = jnp.arange(half_dim).astype(f32)
    frequencies = jnp.power(ROPE_BASE, ladder * (-2.0 / head_dim))
    angles = positions.astype(f32)[..., None] * frequencies
    cosine = jnp.cos(angles)
    sines = jnp.sin(angles)
    cosine = jnp.concatenate([cosine, cosine], axis=-1)
    sines = jnp.concatenate([-sines, sines], axis=-1)

    per_group = w_query.shape[1] // head_dim // kv_dev
    mask = np.zeros((rows_pad, rows_pad), np.float32)
    mask[:total_rows, :total_rows] = allowed
    mask[total_rows:, 0] = 1.0
    mask = jnp.asarray(np.tile(mask, (per_group, 1)))
    qkv = finish_rows(halves, cosine, sines, seq_dev, rows_seq, rows_pad, w_query.shape[1] // head_dim, kv_dev)
    scored, k_here = [], None
    for k in range(kv_dev):
        *pair, k_here = score_head(
            k, qkv, mask, lengths, k_got[k], kv_dev, per_group, k_here
        )
        scored.append(pair)
    done = None
    for k in range(kv_dev):
        done = blend_head(k, *scored[k], lengths, hi, v_got[k], kv_dev, per_group, rows_pad, done)
    attended, v_here = done
    attended = attended[:, :total_rows].reshape(seq_dev * total_rows, w_query.shape[1])
    return (attended, k_here, v_here)


def solution(mesh):
    placed = (
        P(),
        P(),
        P(),
        P("batch"),
        P("batch", "head"),
        P("batch", "head"),
        P("batch", "head"),
        P("batch", "head"),
        P(None, None, ("head", "batch"), None),
        P(None, None, ("head", "batch"), None),
    )
    return jax.shard_map(
        layer,
        mesh=mesh,
        in_specs=placed,
        out_specs=(
            P("batch", "head"),
            P("head", "batch", None, None),
            P("head", "batch", None, None),
        ),
        check_vma=False,
    )
```

time: 622 us -> 407 us (0.65); the launches traced: 621 us -> 400 us
  waiting for transfers between devices: 360 us -> 192 us
  local copies, waits for them, and re-layouts: 99.5 us -> 24.1 us
  Pallas kernels: 0 us -> 73.4 us
  starting transfers between devices: 14.7 us -> 82.5 us
  blocking collectives: 63.5 us -> 0 us
  matrix products: 43.3 us -> 11.9 us
  between operations: 14.8 us -> 1.12 us
  other arithmetic: 24.8 us -> 14.4 us
    all_gather x4 -> x0, waiting for transfers between devices: 228 us -> none  [the longest x1 142 us: per_device(): lax.all_gather(w_query, 'batch', axis=0, tiled=True)]
    ppermute x0 -> x29, waiting for transfers between devices: none -> 156 us  [the longest x17 127 us: swap(): return lax.ppermute(block, 'batch', [(i, i ^ step) for i in range(n_batch)])]
    all_to_all x2 -> x3, waiting for transfers between devices: 130 us -> 36.8 us  [the longest x2 36.8 us: exchange(): lax.all_to_all(shaped, ('head', 'batch'), split_axis=0, concat_axis=0, ti...]
    pallas_call x0 -> x10, Pallas kernels: none -> 73.4 us  [the longest x2 20.6 us: score_head(): pl.pallas_call(kernel, grid=(seq_dev,), out_shape=(jax.ShapeDtypeStruct((...]
    ppermute x0 -> x29, starting transfers between devices: none -> 69.9 us  [the longest x17 35.8 us: swap(): return lax.ppermute(block, 'batch', [(i, i ^ step) for i in range(n_batch)])]
    unnamed x1 -> x0, blocking collectives: 63.5 us -> none
    gather x4 -> x0, local copies, waits for them, and re-layouts: 63 us -> none  [the longest x1 53.6 us: per_device(): jnp.take(embed_table, jnp.clip(local_ids, 0, vocab_rows - 1), axis=0)]
    dot_general x7 -> x2, matrix products: 43.3 us -> 11.9 us  [project(): done = jnp.dot(stacked, weights, preferred_element_type=f32)]
  transfers between devices with their start and end apart: 7 -> 32, of which waited for: 4 -> 14; matrix products, arithmetic and copies ran while one was open for 6% -> 9% of each run, Pallas kernels for 0% -> 12%
where the time goes in v1:
time: 407 us; the launch traced here: 400 us
  waiting for transfers between devices  192 us (47%)
  starting transfers between devices  82.5 us (20%)
  Pallas kernels  73.4 us (18%)
  local copies, waits for them, and re-layouts  24.1 us (6%)
  other arithmetic  14.4 us (4%)
  matrix products  11.9 us (3%)
    ppermute x17, waiting for transfers between devices, swap(): return lax.ppermute(block, 'batch', [(i, i ^ step) for i in range(n_batch)])  127 us
    all_to_all x2, waiting for transfers between devices, exchange(): lax.all_to_all(shaped, ('head', 'batch'), split_axis=0, concat_axis=0, ti...  36.8 us
    ppermute x17, starting transfers between devices, swap(): return lax.ppermute(block, 'batch', [(i, i ^ step) for i in range(n_batch)])  35.8 us
    ppermute x3, waiting for transfers between devices, layer(): up.append(lax.ppermute(up[-1], 'head', right))  24.8 us
    pallas_call x2, Pallas kernels, score_head(): pl.pallas_call(kernel, grid=(seq_dev,), out_shape=(jax.ShapeDtypeStruct((...  20.6 us
    ppermute x6, starting transfers between devices, layer(): v_got[k].append(lax.ppermute(ours, 'head', shift) if d else ours)  17.1 us
    pallas_call x1, Pallas kernels, lookup_rows(): pl.pallas_call(kernel, out_shape=(out, out), in_specs=[smem, smem, smem,...  17 us
    pallas_call x2, Pallas kernels, blend_head(): pl.pallas_call(kernel, grid=(seq_dev,), out_shape=(jax.ShapeDtypeStruct((...  13.3 us
  transfers between devices with their start and end apart: 32, of which 14 were waited for; matrix products, arithmetic and copies ran while one was open for 9% of the time, Pallas kernels for 12%

profile of v1, /device:TPU:0, one launch (start us, length us, event | category | flops | bytes accessed | tf_op | source)
XLA Modules:
  0.0 399.8 jit_solution(14227908341494890842)
XLA Ops:
  5.0 17.0 %lookup.1 = (bf16[704,2048]{1,0:T(8,128)(2,1)}, bf16[704,2048]{1,0:T(8,128)(2,1)}) custom-call(s32[1]{0:T(128)} %bitcast.1.me_ref, s32[32,22]{1,0:T(8,128)} %copy.24.window_ref, s32[32,192]{1,0:T(8,128)} %copy.25.pool_ref, s32[32,7]{1,0:T(8,128)} %copy.26.guess_ref, bf16[1002,8,2048]{2,1,0:T(8,128)(2,1)} %bitcast.149), custom_call_target="tpu_custom_call" | custom-call | flops 10000000000 | bytes 20000000 | tf_op jit(solution)/shard_map/lookup/pallas_call | solution.py:144
  22.9 5.1 %collective-permute-done = bf16[4,176,2048]{2,1,0:T(8,128)(2,1)S(1)} collective-permute-done((bf16[4,176,2048]{2,1,0:T(8,128)(2,1)}, bf16[4,176,2048]{2,1,0:T(8,128)(2,1)S(1)}, u32[]{:S(2)}, u32[]{:S(2)}) %collective-permute-start) | collective-permute-done | bytes 2883616 | tf_op jit(solution)/shard_map/ppermute | solution.py:457
  34.7 8.1 %collective-permute-start.3 = (bf16[1,2,176,1024]{3,2,1,0:T(8,128)(2,1)S(1)}, bf16[1,2,176,1024]{3,2,1,0:T(8,128)(2,1)S(1)}, u32[]{:S(2)}, u32[]{:S(2)}) collective-permute-start(bf16[1,2,176,1024]{3,2,1,0:T(8,128)(2,1)S(1)} %slice_bitcast_fusion.3), channel_id=1, source_target_pairs={{0,4},{1,5},{2,6},{3,7},{4,0},{5,1},{6,2},{7,3},{8,12},{9,13},{10,... | collective-permute-start | bytes 2162696 | tf_op jit(solution)/shard_map/ppermute | solution.py:457
  42.8 8.5 %collective-permute-done.1 = bf16[2,1,176,1024]{3,2,0,1:T(8,128)(2,1)S(1)} collective-permute-done((bf16[2,1,176,1024]{3,2,0,1:T(8,128)(2,1)S(1)}, bf16[2,1,176,1024]{3,2,0,1:T(8,128)(2,1)S(1)}, u32[]{:S(2)}, u32[]{:S(2)}) %collective-permute-start.1) | collective-permute-done | bytes 720928 | tf_op jit(solution)/shard_map/ppermute | solution.py:457
  51.5 8.1 %collective-permute-start.2 = (bf16[1,1,176,1024]{3,2,1,0:T(8,128)(2,1)S(1)}, bf16[1,1,176,1024]{3,2,1,0:T(8,128)(2,1)S(1)}, u32[]{:S(2)}, u32[]{:S(2)}) collective-permute-start(bf16[1,1,176,1024]{3,2,1,0:T(8,128)(2,1)S(1)} %slice_bitcast_fusion.9), channel_id=1, source_target_pairs={{0,4},{1,5},{2,6},{3,7},{4,0},{5,1},{6,2},{7,3},{8,12},{9,13},{10,... | collective-permute-start | bytes 1081352 | tf_op jit(solution)/shard_map/ppermute | solution.py:457
  61.5 6.5 %collective-permute-done.2 = bf16[1,1,176,1024]{3,2,1,0:T(8,128)(2,1)S(1)} collective-permute-done((bf16[1,1,176,1024]{3,2,1,0:T(8,128)(2,1)S(1)}, bf16[1,1,176,1024]{3,2,1,0:T(8,128)(2,1)S(1)}, u32[]{:S(2)}, u32[]{:S(2)}) %collective-permute-start.2) | collective-permute-done | bytes 360480 | tf_op jit(solution)/shard_map/ppermute | solution.py:457
  69.7 3.5 collective-permute-start.8
  74.5 12.9 %collective-permute-done.8.refs_4_ = bf16[176,2048]{1,0:T(8,128)(2,1)S(1)} collective-permute-done((bf16[176,2048]{1,0:T(8,128)(2,1)S(1)}, bf16[176,2048]{1,0:T(8,128)(2,1)S(1)}, u32[]{:S(2)}, u32[]{:S(2)}) %collective-permute-start.8) | collective-permute-done | bytes 720928 | tf_op jit(solution)/shard_map/ppermute | solution.py:487
  87.4 4.4 %collective-permute-start.9 = (bf16[176,2048]{1,0:T(8,128)(2,1)S(1)}, bf16[176,2048]{1,0:T(8,128)(2,1)S(1)}, u32[]{:S(2)}, u32[]{:S(2)}) collective-permute-start(bf16[176,2048]{1,0:T(8,128)(2,1)S(1)} %collective-permute-done.8.refs_4_), channel_id=1, source_target_pairs={{0,8},{8,16},{16,24},{1,9},{9,17},{17,25},{2,10},{10,18},{18,26},{... | collective-permute-start | bytes 2162696 | tf_op jit(solution)/shard_map/ppermute | solution.py:487
  93.1 12.0 %collective-permute-done.9.refs_5_ = bf16[176,2048]{1,0:T(8,128)(2,1)S(1)} collective-permute-done((bf16[176,2048]{1,0:T(8,128)(2,1)S(1)}, bf16[176,2048]{1,0:T(8,128)(2,1)S(1)}, u32[]{:S(2)}, u32[]{:S(2)}) %collective-permute-start.9) | collective-permute-done | bytes 720928 | tf_op jit(solution)/shard_map/ppermute | solution.py:487
  105.1 5.3 %collective-permute-start.10 = (bf16[176,2048]{1,0:T(8,128)(2,1)S(1)}, bf16[176,2048]{1,0:T(8,128)(2,1)}, u32[]{:S(2)}, u32[]{:S(2)}) collective-permute-start(bf16[176,2048]{1,0:T(8,128)(2,1)S(1)} %collective-permute-done.9.refs_5_), channel_id=1, source_target_pairs={{0,8},{8,16},{16,24},{1,9},{9,17},{17,25},{2,10},{10,18},{18,26},{... | collective-permute-start | bytes 2162696 | tf_op jit(solution)/shard_map/ppermute | solution.py:487
  111.6 6.6 %packs.1 = bf16[8,8,4,64,128]{4,3,2,1,0:T(8,128)(2,1)} custom-call(bf16[8,32,64,128]{3,2,1,0:T(8,128)(2,1)} %in_ref.5), custom_call_target="tpu_custom_call" | custom-call | flops 4000000000 | bytes 8000000 | tf_op jit(solution)/shard_map/packs/pallas_call | solution.py:335
  118.3 4.6 %all-to-all-start.2 = ((bf16[8,8,4,64,128]{4,3,2,1,0:T(8,128)(2,1)}), bf16[8,8,4,64,128]{4,3,2,1,0:T(8,128)(2,1)}, u32[]{:S(2)}, u32[]{:S(2)}) async-start(bf16[8,8,4,64,128]{4,3,2,1,0:T(8,128)(2,1)} %packs.1), calls=%async_computation.2 | async-start | bytes 8388608 | tf_op jit(solution)/shard_map/all_to_all | solution.py:446
  123.5 3.8 collective-permute-done.7.refs_0_
  127.4 5.2 %norm.1 = (bf16[176,1024]{1,0:T(8,128)(2,1)}, bf16[176,1024]{1,0:T(8,128)(2,1)}, bf16[176,1024]{1,0:T(8,128)(2,1)}, bf16[176,1024]{1,0:T(8,128)(2,1)}, bf16[176,...) custom-call(s32[2]{0:T(128)} %pad_add_fusion.at_ref, ...), custom_call_target="tpu_custom_call" | custom-call | flops 2000000000 | bytes 8000000 | tf_op jit(solution)/shard_map/norm/pallas_call | solution.py:405
  138.6 39.5 %collective-permute-done.15 = bf16[176,1024]{1,0:T(8,128)(2,1)S(1)} collective-permute-done((bf16[176,1024]{1,0:T(8,128)(2,1)}, bf16[176,1024]{1,0:T(8,128)(2,1)S(1)}, u32[]{:S(2)}, u32[]{:S(2)}) %collective-permute-start.15) | collective-permute-done | bytes 360480 | tf_op jit(solution)/shard_map/ppermute | solution.py:457
  178.2 8.6 %collective-permute-done.17 = bf16[176,1024]{1,0:T(8,128)(2,1)S(1)} collective-permute-done((bf16[176,1024]{1,0:T(8,128)(2,1)}, bf16[176,1024]{1,0:T(8,128)(2,1)S(1)}, u32[]{:S(2)}, u32[]{:S(2)}) %collective-permute-start.17) | collective-permute-done | bytes 360480 | tf_op jit(solution)/shard_map/ppermute | solution.py:457
  186.8 6.8 %convolution_convert_fusion = f16[704,2560]{1,0:T(8,128)(2,1)} fusion(bf16[1024,2560]{1,0:T(8,128)(2,1)S(1)} %constant_dynamic-update-slice_fusion, bf16[176,1024]{1,0:T(8,128)(2,1)S(1)} %collective-permute-done.17, bf16[176,1024]{1,0:T(8,128)(2,1)S(1)} %collective-permute-done.16, bf16[176,1024]{1,0:T(8,128)(2,1)S(1)} %collective-permute-done.15, ...), kind=kOutput, calls=%fused_computation.1 | convolution fusion | flops 3698556928 | bytes 10289152 | tf_op jit(solution)/shard_map/dot_general | solution.py:499
  195.3 3.8 pack.3
  199.0 3.9 pack.2
  206.5 5.0 %all-to-all-start.1 = ((bf16[32,4,64,128]{3,2,1,0:T(8,128)(2,1)}), bf16[32,4,64,128]{3,2,1,0:T(8,128)(2,1)S(1)}, u32[]{:S(2)}, u32[]{:S(2)}) async-start(bf16[32,4,64,128]{3,2,1,0:T(8,128)(2,1)} %bitcast.148), calls=%async_computation.1 | async-start | bytes 4194304 | tf_op jit(solution)/shard_map/all_to_all | solution.py:441
  211.5 3.4 fusion.39
  221.8 8.1 %collective-permute-start.28 = (bf16[8,4,64,128]{3,2,1,0:T(8,128)(2,1)}, bf16[8,4,64,128]{3,2,1,0:T(8,128)(2,1)}, u32[]{:S(2)}, u32[]{:S(2)}) collective-permute-start(bf16[8,4,64,128]{3,2,1,0:T(8,128)(2,1)} %get-tuple-element.51), channel_id=1, source_target_pairs={{0,24},{8,0},{16,8},{24,16},{1,25},{9,1},{17,9},{25,17},{2,26},{10... | collective-permute-start | bytes 1572872 | tf_op jit(solution)/shard_map/ppermute | solution.py:454
  231.1 5.1 %fusion.4 = f32[704,2560]{1,0:T(8,128)S(1)} fusion(bf16[1024,2560]{1,0:T(8,128)(2,1)S(1)} %bitcast.144, bf16[176,1024]{1,0:T(8,128)(2,1)} %collective-permute-done.13, bf16[176,1024]{1,0:T(8,128)(2,1)} %collective-permute-done.12, bf16[176,1024]{1,0:T(8,128)(2,1)} %copy-done.18, bf16[176,1024]{1,0:T(8,128)(2,1)S(1)} %copy-done.19), kind=kOutput, calls=%fused_computation.10 | convolution fusion | flops 3696754688 | bytes 13893632 | tf_op jit(solution)/shard_map/dot_general | solution.py:499
  246.9 36.8 %all-to-all-done.1.k_ref = bf16[32,4,64,128]{3,2,1,0:T(8,128)(2,1)S(1)} async-done(((bf16[32,4,64,128]{3,2,1,0:T(8,128)(2,1)}), bf16[32,4,64,128]{3,2,1,0:T(8,128)(2,1)S(1)}, u32[]{:S(2)}, u32[]{:S(2)}) %all-to-all-start.1) | async-done | bytes 2097184 | tf_op jit(solution)/shard_map/all_to_all | solution.py:441
  293.5 31.3 %collective-permute-done.19 = f16[2,1,176,1280]{3,2,0,1:T(8,128)(2,1)S(1)} collective-permute-done((f16[2,1,176,1280]{3,2,0,1:T(8,128)(2,1)S(1)}, f16[2,1,176,1280]{3,2,0,1:T(8,128)(2,1)S(1)}, u32[]{:S(2)}, u32[]{:S(2)}) %collective-permute-start.19) | collective-permute-done | bytes 901152 | tf_op jit(solution)/shard_map/ppermute | solution.py:457
  325.7 12.7 %collective-permute-done.22 = f16[1,1,176,1280]{3,2,1,0:T(8,128)(2,1)S(1)} collective-permute-done((f16[1,1,176,1280]{3,2,1,0:T(8,128)(2,1)S(1)}, f16[1,1,176,1280]{3,2,1,0:T(8,128)(2,1)S(1)}, u32[]{:S(2)}, u32[]{:S(2)}) %collective-permute-start.22) | collective-permute-done | bytes 450592 | tf_op jit(solution)/shard_map/ppermute | solution.py:457
  340.6 12.3 %collective-permute-done.20 = f16[1,1,176,1280]{3,2,1,0:T(8,128)(2,1)S(1)} collective-permute-done((f16[1,1,176,1280]{3,2,1,0:T(8,128)(2,1)S(1)}, f16[1,1,176,1280]{3,2,1,0:T(8,128)(2,1)S(1)}, u32[]{:S(2)}, u32[]{:S(2)}) %collective-permute-start.20) | collective-permute-done | bytes 450592 | tf_op jit(solution)/shard_map/ppermute | solution.py:457
  361.3 10.3 %score.2 = (bf16[4,4,384,512]{3,2,1,0:T(8,128)(2,1)}, f32[4,384,128]{2,1,0:T(8,128)}, bf16[2,4,2048,128]{3,2,1,0:T(8,128)(2,1)}) custom-call(s32[4]{0:T(128)} %len_ref.7, bf16[4,48,2560]{2,1,0:T(8,128)(2,1)} %finish.1.q_ref.kn_ref.vn_ref, bf16[4,48,2560]{2,1,0:T(8,128)(2,1)} %finish.1.q_ref.kn_ref.vn_ref, bf16[4,48,2560]{2,1,0:T(8,128)(2,1)} %finish.1.q_ref.kn_ref.vn_ref, ...), custom_call_target="tpu_custom_call" | custom-call | flops 2000000000 | bytes 10000000 | tf_op jit(solution)/shard_map/score/pallas_call | solution.py:221
  371.6 6.7 %blend.2 = (bf16[4,48,2048]{2,1,0:T(8,128)(2,1)}, bf16[2,4,2048,128]{3,2,1,0:T(8,128)(2,1)}) custom-call(s32[4]{0:T(128)} %len_ref.7, s32[1]{0:T(128)} %bitcast.at_ref, bf16[4,4,384,512]{3,2,1,0:T(8,128)(2,1)} %get-tuple-element.36.w_ref, f32[4,384,128]{2,1,0:T(8,128)} %get-tuple-element.37.new_ref, bf16[8,4,64,128]{3,2,1,0:T(8,128)(2,1)} %get-tuple-element.54.refs_0_, ...), custom_call_target="tpu_custom_call" | custom-call | flops 1000000000 | bytes 10000000 | tf_op jit(solution)/shard_map/blend/pallas_call | solution.py:284
  379.6 10.3 %score.3 = (bf16[4,4,384,512]{3,2,1,0:T(8,128)(2,1)}, f32[4,384,128]{2,1,0:T(8,128)}, bf16[2,4,2048,128]{3,2,1,0:T(8,128)(2,1)}) custom-call(s32[4]{0:T(128)} %len_ref.7, bf16[4,48,2560]{2,1,0:T(8,128)(2,1)} %finish.1.q_ref.kn_ref.vn_ref, bf16[4,48,2560]{2,1,0:T(8,128)(2,1)} %finish.1.q_ref.kn_ref.vn_ref, ...), custom_call_target="tpu_custom_call", output_to_operand_aliasing={{2}: (6, {})} | custom-call | flops 2000000000 | bytes 10000000 | tf_op jit(solution)/shard_map/score/pallas_call | solution.py:221
  391.0 6.6 %blend.3 = (bf16[4,48,2048]{2,1,0:T(8,128)(2,1)}, bf16[2,4,2048,128]{3,2,1,0:T(8,128)(2,1)}) custom-call(s32[4]{0:T(128)} %len_ref.7, s32[1]{0:T(128)} %bitcast.at_ref, bf16[4,4,384,512]{3,2,1,0:T(8,128)(2,1)} %get-tuple-element.34.w_ref, f32[4,384,128]{2,1,0:T(8,128)} %get-tuple-element.35.new_ref, ...), custom_call_target="tpu_custom_call", output_to_operand_aliasing={{0}: (8, {}), {1}: (9, {})} | custom-call | flops 1000000000 | bytes 10000000 | tf_op jit(solution)/shard_map/blend/pallas_call | solution.py:284
  (128 shorter events, 75.9 us)
Async XLA Ops:
  22.0 5.9 %collective-permute-start = (bf16[4,176,2048]{2,1,0:T(8,128)(2,1)}, bf16[4,176,2048]{2,1,0:T(8,128)(2,1)S(1)}, u32[]{:S(2)}, u32[]{:S(2)}) collective-permute-start(bf16[4,176,2048]{2,1,0:T(8,128)(2,1)} %bitcast.150), channel_id=1, source_target_pairs={{0,1},{1,0},{2,3},{3,2},{4,5},{5,4},{6,7},{7,6},{8,9},{9,8},{10,11... | collective-permute-start | bytes 8650760 | tf_op jit(solution)/shard_map/ppermute | solution.py:457
  31.4 20.0 %collective-permute-start.1 = (bf16[2,1,176,1024]{3,2,0,1:T(8,128)(2,1)S(1)}, bf16[2,1,176,1024]{3,2,0,1:T(8,128)(2,1)S(1)}, u32[]{:S(2)}, u32[]{:S(2)}) collective-permute-start(bf16[2,1,176,1024]{3,2,0,1:T(8,128)(2,1)S(1)} %slice_bitcast_fusion.5), channel_id=1, source_target_pairs={{0,2},{1,3},{2,0},{3,1},{4,6},{5,7},{6,4},{7,5},{8,10},{9,11},{10,... | collective-permute-start | bytes 2162696 | tf_op jit(solution)/shard_map/ppermute | solution.py:457
  34.7 24.8 %collective-permute-start.3 = (bf16[1,2,176,1024]{3,2,1,0:T(8,128)(2,1)S(1)}, bf16[1,2,176,1024]{3,2,1,0:T(8,128)(2,1)S(1)}, u32[]{:S(2)}, u32[]{:S(2)}) collective-permute-start(bf16[1,2,176,1024]{3,2,1,0:T(8,128)(2,1)S(1)} %slice_bitcast_fusion.3), channel_id=1, source_target_pairs={{0,4},{1,5},{2,6},{3,7},{4,0},{5,1},{6,2},{7,3},{8,12},{9,13},{10,... | collective-permute-start | bytes 2162696 | tf_op jit(solution)/shard_map/ppermute | solution.py:457
  51.5 16.5 %collective-permute-start.2 = (bf16[1,1,176,1024]{3,2,1,0:T(8,128)(2,1)S(1)}, bf16[1,1,176,1024]{3,2,1,0:T(8,128)(2,1)S(1)}, u32[]{:S(2)}, u32[]{:S(2)}) collective-permute-start(bf16[1,1,176,1024]{3,2,1,0:T(8,128)(2,1)S(1)} %slice_bitcast_fusion.9), channel_id=1, source_target_pairs={{0,4},{1,5},{2,6},{3,7},{4,0},{5,1},{6,2},{7,3},{8,12},{9,13},{10,... | collective-permute-start | bytes 1081352 | tf_op jit(solution)/shard_map/ppermute | solution.py:457
  59.7 9.9 %collective-permute-start.4 = (bf16[1,1,176,1024]{3,2,1,0:T(8,128)(2,1)S(1)}, bf16[1,1,176,1024]{3,2,1,0:T(8,128)(2,1)S(1)}, u32[]{:S(2)}, u32[]{:S(2)}) collective-permute-start(bf16[1,1,176,1024]{3,2,1,0:T(8,128)(2,1)S(1)} %slice_bitcast_fusion.7), channel_id=1, source_target_pairs={{0,2},{1,3},{2,0},{3,1},{4,6},{5,7},{6,4},{7,5},{8,10},{9,11},{10,... | collective-permute-start | bytes 1081352 | tf_op jit(solution)/shard_map/ppermute | solution.py:457
  69.7 17.7 %collective-permute-start.8 = (bf16[176,2048]{1,0:T(8,128)(2,1)S(1)}, bf16[176,2048]{1,0:T(8,128)(2,1)S(1)}, u32[]{:S(2)}, u32[]{:S(2)}) collective-permute-start(bf16[176,2048]{1,0:T(8,128)(2,1)S(1)} %pad_maximum_fusion.refs_3_), channel_id=1, source_target_pairs={{0,8},{8,16},{16,24},{1,9},{9,17},{17,25},{2,10},{10,18},{18,26},{... | collective-permute-start | bytes 2162696 | tf_op jit(solution)/shard_map/ppermute | solution.py:487
  73.2 18.6 %collective-permute-start.5 = (bf16[176,2048]{1,0:T(8,128)(2,1)S(1)}, bf16[176,2048]{1,0:T(8,128)(2,1)S(1)}, u32[]{:S(2)}, u32[]{:S(2)}) collective-permute-start(bf16[176,2048]{1,0:T(8,128)(2,1)S(1)} %pad_maximum_fusion.refs_3_), channel_id=1, source_target_pairs={{8,0},{16,8},{24,16},{9,1},{17,9},{25,17},{10,2},{18,10},{26,18},{... | collective-permute-start | bytes 2162696 | tf_op jit(solution)/shard_map/ppermute | solution.py:488
  87.4 17.7 %collective-permute-start.9 = (bf16[176,2048]{1,0:T(8,128)(2,1)S(1)}, bf16[176,2048]{1,0:T(8,128)(2,1)S(1)}, u32[]{:S(2)}, u32[]{:S(2)}) collective-permute-start(bf16[176,2048]{1,0:T(8,128)(2,1)S(1)} %collective-permute-done.8.refs_4_), channel_id=1, source_target_pairs={{0,8},{8,16},{16,24},{1,9},{9,17},{17,25},{2,10},{10,18},{18,26},{... | collective-permute-start | bytes 2162696 | tf_op jit(solution)/shard_map/ppermute | solution.py:487
  91.8 18.5 %collective-permute-start.6 = (bf16[176,2048]{1,0:T(8,128)(2,1)S(1)}, bf16[176,2048]{1,0:T(8,128)(2,1)}, u32[]{:S(2)}, u32[]{:S(2)}) collective-permute-start(bf16[176,2048]{1,0:T(8,128)(2,1)S(1)} %collective-permute-done.5.refs_2_), channel_id=1, source_target_pairs={{8,0},{16,8},{24,16},{9,1},{17,9},{25,17},{10,2},{18,10},{26,18},{... | collective-permute-start | bytes 2162696 | tf_op jit(solution)/shard_map/ppermute | solution.py:488
  105.1 18.4 %collective-permute-start.10 = (bf16[176,2048]{1,0:T(8,128)(2,1)S(1)}, bf16[176,2048]{1,0:T(8,128)(2,1)}, u32[]{:S(2)}, u32[]{:S(2)}) collective-permute-start(bf16[176,2048]{1,0:T(8,128)(2,1)S(1)} %collective-permute-done.9.refs_5_), channel_id=1, source_target_pairs={{0,8},{8,16},{16,24},{1,9},{9,17},{17,25},{2,10},{10,18},{18,26},{... | collective-permute-start | bytes 2162696 | tf_op jit(solution)/shard_map/ppermute | solution.py:487
  110.4 17.0 %collective-permute-start.7 = (bf16[176,2048]{1,0:T(8,128)(2,1)}, bf16[176,2048]{1,0:T(8,128)(2,1)}, u32[]{:S(2)}, u32[]{:S(2)}) collective-permute-start(bf16[176,2048]{1,0:T(8,128)(2,1)} %collective-permute-done.6.refs_1_), channel_id=1, source_target_pairs={{8,0},{16,8},{24,16},{9,1},{17,9},{25,17},{10,2},{18,10},{26,18},{... | collective-permute-start | bytes 2162696 | tf_op jit(solution)/shard_map/ppermute | solution.py:488
  118.3 88.2 %all-to-all-start.2 = ((bf16[8,8,4,64,128]{4,3,2,1,0:T(8,128)(2,1)}), bf16[8,8,4,64,128]{4,3,2,1,0:T(8,128)(2,1)}, u32[]{:S(2)}, u32[]{:S(2)}) async-start(bf16[8,8,4,64,128]{4,3,2,1,0:T(8,128)(2,1)} %packs.1), calls=%async_computation.2 | async-start | bytes 8388608 | tf_op jit(solution)/shard_map/all_to_all | solution.py:446
  132.6 6.0 %collective-permute-start.14 = (bf16[176,1024]{1,0:T(8,128)(2,1)}, bf16[176,1024]{1,0:T(8,128)(2,1)S(1)}, u32[]{:S(2)}, u32[]{:S(2)}) collective-permute-start(bf16[176,1024]{1,0:T(8,128)(2,1)} %get-tuple-element.29), channel_id=1, source_target_pairs={{0,1},{1,0},{2,3},{3,2},{4,5},{5,4},{6,7},{7,6},{8,9},{9,8},{10,11... | collective-permute-start | bytes 1081352 | tf_op jit(solution)/shard_map/ppermute | solution.py:457
  132.6 45.5 %collective-permute-start.15 = (bf16[176,1024]{1,0:T(8,128)(2,1)}, bf16[176,1024]{1,0:T(8,128)(2,1)S(1)}, u32[]{:S(2)}, u32[]{:S(2)}) collective-permute-start(bf16[176,1024]{1,0:T(8,128)(2,1)} %get-tuple-element.30), channel_id=1, source_target_pairs={{0,3},{1,2},{2,1},{3,0},{4,7},{5,6},{6,5},{7,4},{8,11},{9,10},{10,... | collective-permute-start | bytes 1081352 | tf_op jit(solution)/shard_map/ppermute | solution.py:457
  133.3 44.8 %collective-permute-start.16 = (bf16[176,1024]{1,0:T(8,128)(2,1)}, bf16[176,1024]{1,0:T(8,128)(2,1)S(1)}, u32[]{:S(2)}, u32[]{:S(2)}) collective-permute-start(bf16[176,1024]{1,0:T(8,128)(2,1)} %get-tuple-element.31), channel_id=1, source_target_pairs={{0,5},{1,4},{2,7},{3,6},{4,1},{5,0},{6,3},{7,2},{8,13},{9,12},{10,... | collective-permute-start | bytes 1081352 | tf_op jit(solution)/shard_map/ppermute | solution.py:457
  134.2 52.6 %collective-permute-start.17 = (bf16[176,1024]{1,0:T(8,128)(2,1)}, bf16[176,1024]{1,0:T(8,128)(2,1)S(1)}, u32[]{:S(2)}, u32[]{:S(2)}) collective-permute-start(bf16[176,1024]{1,0:T(8,128)(2,1)} %get-tuple-element.32), channel_id=1, source_target_pairs={{0,7},{1,6},{2,5},{3,4},{4,3},{5,2},{6,1},{7,0},{8,15},{9,14},{10,... | collective-permute-start | bytes 1081352 | tf_op jit(solution)/shard_map/ppermute | solution.py:457
  193.6 42.6 %collective-permute-start.18 = (f16[4,176,2560]{2,1,0:T(8,128)(2,1)}, f16[4,176,2560]{2,1,0:T(8,128)(2,1)}, u32[]{:S(2)}, u32[]{:S(2)}) collective-permute-start(f16[4,176,2560]{2,1,0:T(8,128)(2,1)} %bitcast.20), channel_id=1, source_target_pairs={{0,1},{1,0},{2,3},{3,2},{4,5},{5,4},{6,7},{7,6},{8,9},{9,8},{10,11... | collective-permute-start | bytes 10813448 | tf_op jit(solution)/shard_map/ppermute | solution.py:457
  203.0 16.4 %collective-permute-start.11 = (bf16[176,1024]{1,0:T(8,128)(2,1)S(1)}, bf16[176,1024]{1,0:T(8,128)(2,1)S(1)}, u32[]{:S(2)}, u32[]{:S(2)}) collective-permute-start(bf16[176,1024]{1,0:T(8,128)(2,1)S(1)} %copy-done.17), channel_id=1, source_target_pairs={{0,2},{1,3},{2,0},{3,1},{4,6},{5,7},{6,4},{7,5},{8,10},{9,11},{10,... | collective-permute-start | bytes 1081352 | tf_op jit(solution)/shard_map/ppermute | solution.py:457
  203.5 18.3 %collective-permute-start.12 = (bf16[176,1024]{1,0:T(8,128)(2,1)S(1)}, bf16[176,1024]{1,0:T(8,128)(2,1)}, u32[]{:S(2)}, u32[]{:S(2)}) collective-permute-start(bf16[176,1024]{1,0:T(8,128)(2,1)S(1)} %copy-done.16), channel_id=1, source_target_pairs={{0,4},{1,5},{2,6},{3,7},{4,0},{5,1},{6,2},{7,3},{8,12},{9,13},{10,... | collective-permute-start | bytes 1081352 | tf_op jit(solution)/shard_map/ppermute | solution.py:457
  204.0 26.6 %collective-permute-start.13 = (bf16[176,1024]{1,0:T(8,128)(2,1)S(1)}, bf16[176,1024]{1,0:T(8,128)(2,1)}, u32[]{:S(2)}, u32[]{:S(2)}) collective-permute-start(bf16[176,1024]{1,0:T(8,128)(2,1)S(1)} %copy-done.15), channel_id=1, source_target_pairs={{0,6},{1,7},{2,4},{3,5},{4,2},{5,3},{6,0},{7,1},{8,14},{9,15},{10,... | collective-permute-start | bytes 1081352 | tf_op jit(solution)/shard_map/ppermute | solution.py:457
  206.5 77.2 %all-to-all-start.1 = ((bf16[32,4,64,128]{3,2,1,0:T(8,128)(2,1)}), bf16[32,4,64,128]{3,2,1,0:T(8,128)(2,1)S(1)}, u32[]{:S(2)}, u32[]{:S(2)}) async-start(bf16[32,4,64,128]{3,2,1,0:T(8,128)(2,1)} %bitcast.148), calls=%async_computation.1 | async-start | bytes 4194304 | tf_op jit(solution)/shard_map/all_to_all | solution.py:441
  216.2 140.3 %collective-permute-start.26 = (bf16[8,4,64,128]{3,2,1,0:T(8,128)(2,1)}, bf16[8,4,64,128]{3,2,1,0:T(8,128)(2,1)}, u32[]{:S(2)}, u32[]{:S(2)}) collective-permute-start(bf16[8,4,64,128]{3,2,1,0:T(8,128)(2,1)} %get-tuple-element.53), channel_id=1, source_target_pairs={{0,8},{8,16},{16,24},{24,0},{1,9},{9,17},{17,25},{25,1},{2,10},{10... | collective-permute-start | bytes 1572872 | tf_op jit(solution)/shard_map/ppermute | solution.py:454
  219.4 152.3 %collective-permute-start.27 = (bf16[8,4,64,128]{3,2,1,0:T(8,128)(2,1)}, bf16[8,4,64,128]{3,2,1,0:T(8,128)(2,1)}, u32[]{:S(2)}, u32[]{:S(2)}) collective-permute-start(bf16[8,4,64,128]{3,2,1,0:T(8,128)(2,1)} %get-tuple-element.52), channel_id=1, source_target_pairs={{0,16},{8,24},{16,0},{24,8},{1,17},{9,25},{17,1},{25,9},{2,18},{10... | collective-permute-start | bytes 1572872 | tf_op jit(solution)/shard_map/ppermute | solution.py:454
  221.8 149.9 %collective-permute-start.28 = (bf16[8,4,64,128]{3,2,1,0:T(8,128)(2,1)}, bf16[8,4,64,128]{3,2,1,0:T(8,128)(2,1)}, u32[]{:S(2)}, u32[]{:S(2)}) collective-permute-start(bf16[8,4,64,128]{3,2,1,0:T(8,128)(2,1)} %get-tuple-element.51), channel_id=1, source_target_pairs={{0,24},{8,0},{16,8},{24,16},{1,25},{9,1},{17,9},{25,17},{2,26},{10... | collective-permute-start | bytes 1572872 | tf_op jit(solution)/shard_map/ppermute | solution.py:454
  230.5 159.4 %collective-permute-start.23 = (bf16[8,4,64,128]{3,2,1,0:T(8,128)(2,1)}, bf16[8,4,64,128]{3,2,1,0:T(8,128)(2,1)S(1)}, u32[]{:S(2)}, u32[]{:S(2)}) collective-permute-start(bf16[8,4,64,128]{3,2,1,0:T(8,128)(2,1)} %get-tuple-element.57), channel_id=1, source_target_pairs={{0,8},{8,16},{16,24},{24,0},{1,9},{9,17},{17,25},{25,1},{2,10},{10... | collective-permute-start | bytes 1572872 | tf_op jit(solution)/shard_map/ppermute | solution.py:454
  242.2 47.4 %collective-permute-start.21 = (f16[1,2,176,1280]{3,2,1,0:T(8,128)(2,1)S(1)}, f16[1,2,176,1280]{3,2,1,0:T(8,128)(2,1)}, u32[]{:S(2)}, u32[]{:S(2)}) collective-permute-start(f16[1,2,176,1280]{3,2,1,0:T(8,128)(2,1)S(1)} %fusion.19), channel_id=1, source_target_pairs={{0,4},{1,5},{2,6},{3,7},{4,0},{5,1},{6,2},{7,3},{8,12},{9,13},{10,... | collective-permute-start | bytes 2703368 | tf_op jit(solution)/shard_map/ppermute | solution.py:457
  285.0 93.3 %all-to-all-start = ((bf16[32,4,64,128]{3,2,1,0:T(8,128)(2,1)}), bf16[32,4,64,128]{3,2,1,0:T(8,128)(2,1)S(1)}, u32[]{:S(2)}, u32[]{:S(2)}) async-start(bf16[32,4,64,128]{3,2,1,0:T(8,128)(2,1)} %bitcast.147), calls=%async_computation | async-start | bytes 4194304 | tf_op jit(solution)/shard_map/all_to_all | solution.py:441
  289.5 35.3 %collective-permute-start.19 = (f16[2,1,176,1280]{3,2,0,1:T(8,128)(2,1)S(1)}, f16[2,1,176,1280]{3,2,0,1:T(8,128)(2,1)S(1)}, u32[]{:S(2)}, u32[]{:S(2)}) collective-permute-start(f16[2,1,176,1280]{3,2,0,1:T(8,128)(2,1)S(1)} %fusion.20), channel_id=1, source_target_pairs={{0,2},{1,3},{2,0},{3,1},{4,6},{5,7},{6,4},{7,5},{8,10},{9,11},{10,... | collective-permute-start | bytes 2703368 | tf_op jit(solution)/shard_map/ppermute | solution.py:457
  324.8 13.5 %collective-permute-start.22 = (f16[1,1,176,1280]{3,2,1,0:T(8,128)(2,1)S(1)}, f16[1,1,176,1280]{3,2,1,0:T(8,128)(2,1)S(1)}, u32[]{:S(2)}, u32[]{:S(2)}) collective-permute-start(f16[1,1,176,1280]{3,2,1,0:T(8,128)(2,1)S(1)} %fusion.30), channel_id=1, source_target_pairs={{0,2},{1,3},{2,0},{3,1},{4,6},{5,7},{6,4},{7,5},{8,10},{9,11},{10,... | collective-permute-start | bytes 1351688 | tf_op jit(solution)/shard_map/ppermute | solution.py:457
  338.3 14.6 %collective-permute-start.20 = (f16[1,1,176,1280]{3,2,1,0:T(8,128)(2,1)S(1)}, f16[1,1,176,1280]{3,2,1,0:T(8,128)(2,1)S(1)}, u32[]{:S(2)}, u32[]{:S(2)}) collective-permute-start(f16[1,1,176,1280]{3,2,1,0:T(8,128)(2,1)S(1)} %fusion.29), channel_id=1, source_target_pairs={{0,4},{1,5},{2,6},{3,7},{4,0},{5,1},{6,2},{7,3},{8,12},{9,13},{10,... | collective-permute-start | bytes 1351688 | tf_op jit(solution)/shard_map/ppermute | solution.py:457
  352.9 37.0 %collective-permute-start.24 = (bf16[8,4,64,128]{3,2,1,0:T(8,128)(2,1)}, bf16[8,4,64,128]{3,2,1,0:T(8,128)(2,1)S(1)}, u32[]{:S(2)}, u32[]{:S(2)}) collective-permute-start(bf16[8,4,64,128]{3,2,1,0:T(8,128)(2,1)} %get-tuple-element.56), channel_id=1, source_target_pairs={{0,16},{8,24},{16,0},{24,8},{1,17},{9,25},{17,1},{25,9},{2,18},{10... | collective-permute-start | bytes 1572872 | tf_op jit(solution)/shard_map/ppermute | solution.py:454
  356.5 33.5 %collective-permute-start.25 = (bf16[8,4,64,128]{3,2,1,0:T(8,128)(2,1)}, bf16[8,4,64,128]{3,2,1,0:T(8,128)(2,1)}, u32[]{:S(2)}, u32[]{:S(2)}) collective-permute-start(bf16[8,4,64,128]{3,2,1,0:T(8,128)(2,1)} %get-tuple-element.55), channel_id=1, source_target_pairs={{0,24},{8,0},{16,8},{24,16},{1,25},{9,1},{17,9},{25,17},{2,26},{10... | collective-permute-start | bytes 1572872 | tf_op jit(solution)/shard_map/ppermute | solution.py:454
  (22 other events, 410.7 us)
